TPU v7x, 32 devices: a whole 2x2x4 slice. The times are simulated.
32 devices in a mesh: ep: 4 (over y, x), grp: 8 (over z, core).
Axes of the slice: x: 2, y: 2, z: 4, core: 2. Of those that a mesh axis runs over, the one named last changes fastest.
Arguments:
- tokens: bfloat16 [4096, 4096], P(('ep', 'grp')), may hold values from -6 to 6
- expert_ids: int32 [4096, 8], P(('ep', 'grp')), may hold values from 0 to 127, all different within a row; in each aligned block of 128 rows (0 to 127, 128 to 255, ...) at most 16 rows name the same one
- combine: float32 [4096, 8], P(('ep', 'grp')), may hold values from 0.05 to 1
- w_gate: bfloat16 [4096, 1280], P(None, 'ep'), may hold values from -0.09375 to 0.09375
- w_up: bfloat16 [4096, 1280], P(None, 'ep'), may hold values from -0.09375 to 0.09375
- w_down: bfloat16 [1280, 4096], P('ep'), may hold values from -0.15625 to 0.15625
- bias: float32 [128], replicated, may hold values from -3 to 3
Outputs:
- mixed: bfloat16 [4096, 4096], P(('ep', 'grp'))
- new_bias: float32 [128], replicated
Inputs may be any that keep to these rules, and one draw needn't show every extreme that they name: `expert_ids`: each row names 8 different experts. Among the rows of one device no expert is named more than 16 times, a bound that some block reaches.
All inputs are finite; a program needn't handle non-finite values.
Results may differ from a plain program's by a relative error of at most 0.0057.
Values may be sent and summed in bfloat16 or wider, within the bound.
A program may use at most 64 MiB of HBM per device.

v0:
```python
import jax
import jax.numpy as jnp
from jax import lax
from jax.sharding import PartitionSpec as P

NEXP = 128
TOPK = 8
SPLIT = 4


def count_loads(expert_ids):
    experts = jnp.arange(NEXP, dtype=jnp.int32)
    local = jnp.sum(
        (expert_ids.reshape(-1)[:, None] == experts[None, :]).astype(jnp.float32), axis=0
    )
    within = lax.psum(local, "ep")
    return lax.psum(within, "grp")


def per_device(tokens, expert_ids, combine, w_gate, w_up, w_down, bias):
    n_ep = lax.axis_size("ep")
    n_grp = lax.axis_size("grp")
    tok_rows = tokens.shape[0]
    width = tokens.shape[1]
    capacity = tok_rows // 8
    win_experts = n_ep // SPLIT
    flat_ids = expert_ids.reshape(-1)
    window = jnp.arange(win_experts, dtype=jnp.int32)
    hit = (flat_ids[:, None] == window[None, :]).astype(jnp.int32)
    ranks = jnp.cumsum(hit, axis=0) - 1
    slot = jnp.sum(hit * ranks, axis=1)
    inside = jnp.sum(hit, axis=1)
    dest = jnp.where(inside > 0, flat_ids * capacity + slot, win_experts * capacity)
    slot_ids = jnp.arange(win_experts * capacity, dtype=jnp.int32)
    chosen = (slot_ids[:, None] == dest[None, :]).reshape(win_experts * capacity, tok_rows, TOPK)
    select = jnp.sum(chosen.astype(jnp.float32), axis=2)
    weights = jnp.sum(chosen.astype(jnp.float32) * combine[None, :, :], axis=2)
    buffer = jnp.dot(
        select.astype(jnp.bfloat16), tokens, preferred_element_type=jnp.float32
    ).astype(jnp.bfloat16)
    outgoing = jnp.repeat(buffer.reshape(win_experts, capacity, width), SPLIT, axis=0)
    block = lax.all_to_all(outgoing, "ep", split_axis=0, concat_axis=0, tiled=True)
    rows = block.reshape(-1, width)
    gate = jnp.dot(rows, w_gate, preferred_element_type=jnp.float32)
    upval = jnp.dot(rows, w_up, preferred_element_type=jnp.float32)
    hidden = (jax.nn.silu(gate) * upval).astype(jnp.bfloat16)
    part = jnp.dot(hidden, w_down, preferred_element_type=jnp.float32).astype(jnp.bfloat16)
    returned = lax.all_to_all(
        part.reshape(block.shape), "ep", split_axis=0, concat_axis=0, tiled=True
    )
    summed = jnp.sum(
        returned.astype(jnp.float32).reshape(win_experts, SPLIT, capacity, width), axis=1
    )
    summed = summed.reshape(win_experts * capacity, width)
    mixed = jnp.dot(
        weights.T, summed, precision=lax.Precision.HIGHEST, preferred_element_type=jnp.float32
    ).astype(jnp.bfloat16)
    load = count_loads(expert_ids)
    mean_load = jnp.float32(tok_rows * n_ep * n_grp * TOPK / NEXP)
    new_bias = bias - 0.05 * (load - mean_load) / jnp.sqrt(mean_load)
    return (mixed, new_bias)


def solution(mesh):
    return jax.shard_map(
        per_device,
        mesh=mesh,
        in_specs=(
            P(("ep", "grp"), None),
            P(("ep", "grp"), None),
            P(("ep", "grp"), None),
            P(None, "ep"),
            P(None, "ep"),
            P("ep", None),
            P(),
        ),
        out_specs=(P(("ep", "grp"), None), P()),
        check_vma=False,
    )
```

profile of v0, /device:TPU:0, one launch (start us, length us, event | category | flops | bytes accessed | tf_op | source)
XLA Modules:
  0.0 56.3 jit_solution(11772067957491407302)
XLA Ops:
  0.6 0.8 %fusion.8 = s32[128,8]{0,1:T(8,128)S(1)} fusion(s32[128,8]{0,1:T(8,128)} %param.8), kind=kLoop, calls=%fused_computation.21 | loop fusion | flops 2048 | bytes 8192 | tf_op jit(solution)/shard_map/convert_element_type | solution.py:29
  1.5 0.1 copy.30
  1.6 0.1 reshape.124
  1.7 0.3 reduce-window.6
  2.0 0.2 slice_reduce_fusion
  2.2 0.1 reshape.117
  2.2 0.2 reduce-window.9
  2.4 0.1 broadcast.76
  2.5 0.1 reshape.120
  2.7 0.9 %add_select_fusion = s32[128,8]{0,1:T(8,128)S(1)} fusion(s32[128,8]{0,1:T(8,128)S(1)} %copy.31, s32[128,8]{0,1:T(8,128)S(1)} %copy.32, s32[128,8]{0,1:T(8,128)} %param.8), kind=kLoop, calls=%fused_computation.18 | loop fusion | flops 9216 | bytes 16384 | tf_op jit(solution)/shard_map/jit(_where)/select_n | solution.py:33
  3.6 0.7 %convert_reduce_fusion.2 = (bf16[16,128]{1,0:T(8,128)(2,1)S(1)}, f32[16,128]{1,0:T(8,128)S(1)}) fusion(s32[128,8]{0,1:T(8,128)S(1)} %add_select_fusion, f32[128,8]{0,1:T(8,128)} %param.9), kind=kLoop, calls=%fused_computation.13 | loop fusion | flops 77824 | bytes 20480 | tf_op jit(solution)/shard_map/reduce_sum | solution.py:36
  4.3 1.5 %convolution_convert_fusion.2 = bf16[16,4096]{1,0:T(8,128)(2,1)S(1)} fusion(bf16[128,4096]{1,0:T(8,128)(2,1)} %param.7, bf16[16,128]{1,0:T(8,128)(2,1)S(1)} %get-tuple-element.2), kind=kOutput, calls=%fused_computation.2 | convolution fusion | flops 16842752 | bytes 1183744 | tf_op jit(solution)/shard_map/dot_general | solution.py:38
  5.8 13.5 %all_to_all.10 = bf16[4,16,4096]{2,1,0:T(8,128)(2,1)S(1)} all-to-all(bf16[4,16,4096]{2,1,0:T(8,128)(2,1)S(1)} %reshape.121), channel_id=1, replica_groups=mesh['ep'=4,'grp'=8] {'ep'}, dimensions={0} | all-to-all | bytes 1048576 | tf_op jit(solution)/shard_map/all_to_all | solution.py:42
  19.3 0.9 %fusion.10 = f32[64,320]{1,0:T(8,128)S(1)} fusion(bf16[64,4096]{1,0:T(8,128)(2,1)S(1)} %bitcast.16, bf16[4096,320]{0,1:T(8,128)(2,1)S(1)} %copy-done.1), kind=kOutput, calls=%fused_computation.25 | convolution fusion | flops 167772160 | bytes 3227648 | tf_op jit(solution)/shard_map/dot_general | solution.py:44
  20.3 4.7 %convolution_convert_fusion.1 = bf16[64,4096]{1,0:T(8,128)(2,1)} fusion(bf16[320,4096]{1,0:T(8,128)(2,1)S(1)} %copy-done, bf16[64,4096]{1,0:T(8,128)(2,1)S(1)} %bitcast.17, bf16[4096,320]{0,1:T(8,128)(2,1)} %param.11, f32[64,320]{1,0:T(8,128)S(1)} %fusion.10), kind=kOutput, calls=%fused_computation.1 | convolution fusion | flops 335929344 | bytes 6373376 | tf_op jit(solution)/shard_map/dot_general | solution.py:47
  25.0 3.5 %all-to-all-start.1 = ((bf16[4,16,4096]{2,1,0:T(8,128)(2,1)}), bf16[4,16,4096]{2,1,0:T(8,128)(2,1)S(1)}, u32[]{:S(2)}, u32[]{:S(2)}) async-start(bf16[4,16,4096]{2,1,0:T(8,128)(2,1)} %bitcast.18), calls=%async_computation.1 | async-start | bytes 1048576 | tf_op jit(solution)/shard_map/all_to_all | solution.py:48
  28.5 0.1 copy.33
  28.6 0.1 eq.58
  28.7 0.2 convert_reduce_fusion.1
  28.9 10.4 %psum.14 = f32[128]{0:T(128)S(1)} all-reduce(f32[128]{0:T(128)S(1)} %convert_reduce_fusion.1), channel_id=1, replica_groups=mesh['ep'=4,'grp'=8] {'ep'}, use_global_device_ids=true, to_apply=%region_6.7 | all-reduce | flops 128 | bytes 1024 | tf_op jit(solution)/shard_map/psum | solution.py:16
  39.3 13.6 %psum.15 = f32[128]{0:T(128)S(1)} all-reduce(f32[128]{0:T(128)S(1)} %psum.14), channel_id=1, replica_groups=mesh['ep'=4,'grp'=8] {'grp'}, use_global_device_ids=true, to_apply=%region_7.8 | all-reduce | flops 128 | bytes 1024 | tf_op jit(solution)/shard_map/psum | solution.py:17
  52.9 0.5 multiply_subtract_fusion
  53.4 0.1 convert_reduce_fusion
  53.5 2.8 %convolution_convert_fusion = bf16[128,4096]{1,0:T(8,128)(2,1)} fusion(f32[16,128]{1,0:T(8,128)S(1)} %get-tuple-element.3, f32[16,4096]{1,0:T(8,128)S(1)} %convert_reduce_fusion), kind=kOutput, calls=%fused_computation | convolution fusion | flops 101187584 | bytes 1318912 | tf_op jit(solution)/shard_map/dot_general | solution.py:55
  (13 shorter events, 0.2 us)
Async XLA Ops:
  0.6 19.6 %copy-start = (bf16[320,4096]{1,0:T(8,128)(2,1)S(1)}, bf16[320,4096]{1,0:T(8,128)(2,1)}, u32[]{:S(2)}) copy-start(bf16[320,4096]{1,0:T(8,128)(2,1)} %param.12) | copy-start | bytes 7864324
  2.7 16.6 %copy-start.1 = (bf16[4096,320]{0,1:T(8,128)(2,1)S(1)}, bf16[4096,320]{0,1:T(8,128)(2,1)}, u32[]{:S(2)}) copy-start(bf16[4096,320]{0,1:T(8,128)(2,1)} %param.10) | copy-start | bytes 7864324
  20.2 8.2 %copy-start.2 = (s32[128,8]{0,1:T(8,128)S(1)}, s32[128,8]{0,1:T(8,128)}, u32[]{:S(2)}) copy-start(s32[128,8]{0,1:T(8,128)} %param.8) | copy-start | bytes 12292
  20.3 32.6 %copy-start.3 = (f32[128]{0:T(128)S(1)}, f32[128]{0:T(128)}, u32[]{:S(2)}) copy-start(f32[128]{0:T(128)} %param.13) | copy-start | bytes 1540
  25.0 28.4 %all-to-all-start.1 = ((bf16[4,16,4096]{2,1,0:T(8,128)(2,1)}), bf16[4,16,4096]{2,1,0:T(8,128)(2,1)S(1)}, u32[]{:S(2)}, u32[]{:S(2)}) async-start(bf16[4,16,4096]{2,1,0:T(8,128)(2,1)} %bitcast.18), calls=%async_computation.1 | async-start | bytes 1048576 | tf_op jit(solution)/shard_map/all_to_all | solution.py:48
where the time goes:
time: 56.6 us; the launch traced here: 56.3 us
  blocking collectives  37.5 us (66%)
  matrix products  9.9 us (17%)
  other arithmetic  3.71 us (7%)
  starting transfers between devices  3.47 us (6%)
  local copies, waits for them, and re-layouts  1 us (2%)
  between operations  0.72 us (1%)
    psum x1, blocking collectives, count_loads(): return lax.psum(within, 'grp')  13.6 us
    all_to_all x1, blocking collectives, per_device(): lax.all_to_all(outgoing, 'ep', split_axis=0, concat_axis=0, tiled=True)  13.5 us
    psum x1, blocking collectives, count_loads(): within = lax.psum(local, 'ep')  10.4 us
    dot_general x1, matrix products, per_device(): jnp.dot(hidden, w_down, preferred_element_type=jnp.float32)  4.74 us
    all_to_all x1, starting transfers between devices, per_device(): lax.all_to_all(part.reshape(block.shape), 'ep', split_axis=0, concat_axis...  3.47 us
    dot_general x1, matrix products, per_device(): jnp.dot(weights.T, summed, precision=lax.Precision.HIGHEST, preferred_ele...  2.81 us
    dot_general x1, matrix products, per_device(): jnp.dot(select.astype(jnp.bfloat16), tokens, preferred_element_type=jnp.f...  1.47 us
  transfers between devices with their start and end apart: 1, of which 0 were waited for; matrix products, arithmetic and copies ran while one was open for 2% of the time, Pallas kernels for 0%

commit v1 on v0

--- a/solution.py
+++ b/solution.py
@@ -2,10 +2,15 @@
 import jax.numpy as jnp
 from jax import lax
 from jax.sharding import PartitionSpec as P
+from jax.lax import all_gather
 
 NEXP = 128
 TOPK = 8
 SPLIT = 4
+
+
+def divide_patches(inputs):
+    return jnp.sum(all_gather(inputs, "ep"), axis=0)
 
 
 def count_loads(expert_ids):
@@ -13,7 +18,7 @@
     local = jnp.sum(
         (expert_ids.reshape(-1)[:, None] == experts[None, :]).astype(jnp.float32), axis=0
     )
-    within = lax.psum(local, "ep")
+    within = divide_patches(local)
     return lax.psum(within, "grp")
 
 

time: 56.6 us -> 54.9 us (0.970)
  blocking collectives: 37.5 us -> 35.7 us
    psum x1 -> x0, blocking collectives: 10.4 us -> none  [count_loads(): within = lax.psum(local, 'ep')]
    all_gather x0 -> x1, blocking collectives: none -> 8.46 us  [divide_patches(): return jnp.sum(all_gather(inputs, 'ep'), axis=0)]
where the time goes in v1:
time: 54.9 us; the launch traced here: 54.6 us
  blocking collectives  35.7 us (65%)
  matrix products  9.9 us (18%)
  other arithmetic  3.73 us (7%)
  starting transfers between devices  3.47 us (6%)
  local copies, waits for them, and re-layouts  1 us (2%)
  between operations  0.73 us (1%)
    psum x1, blocking collectives, count_loads(): return lax.psum(within, 'grp')  13.8 us
    all_to_all x1, blocking collectives, per_device(): lax.all_to_all(outgoing, 'ep', split_axis=0, concat_axis=0, tiled=True)  13.5 us
    all_gather x1, blocking collectives, divide_patches(): return jnp.sum(all_gather(inputs, 'ep'), axis=0)  8.46 us
    dot_general x1, matrix products, per_device(): jnp.dot(hidden, w_down, preferred_element_type=jnp.float32)  4.74 us
    all_to_all x1, starting transfers between devices, per_device(): lax.all_to_all(part.reshape(block.shape), 'ep', split_axis=0, concat_axis...  3.47 us
    dot_general x1, matrix products, per_device(): jnp.dot(weights.T, summed, precision=lax.Precision.HIGHEST, preferred_ele...  2.81 us
    dot_general x1, matrix products, per_device(): jnp.dot(select.astype(jnp.bfloat16), tokens, preferred_element_type=jnp.f...  1.47 us
  transfers between devices with their start and end apart: 1, of which 0 were waited for; matrix products, arithmetic and copies ran while one was open for 2% of the time, Pallas kernels for 0%

profile of v1, /device:TPU:0, one launch (start us, length us, event | category | flops | bytes accessed | tf_op | source)
XLA Modules:
  0.0 54.6 jit_solution(14192899444050284648)
XLA Ops:
  0.6 0.8 %fusion.8 = s32[128,8]{0,1:T(8,128)S(1)} fusion(s32[128,8]{0,1:T(8,128)} %param.8), kind=kLoop, calls=%fused_computation.21 | loop fusion | flops 2048 | bytes 8192 | tf_op jit(solution)/shard_map/convert_element_type | solution.py:34
  1.5 0.1 copy.40
  1.6 0.1 reshape.124
  1.7 0.3 reduce-window.6
  2.0 0.2 slice_reduce_fusion
  2.2 0.1 reshape.117
  2.2 0.2 reduce-window.9
  2.4 0.1 broadcast.76
  2.5 0.1 reshape.120
  2.7 0.9 %add_select_fusion = s32[128,8]{0,1:T(8,128)S(1)} fusion(s32[128,8]{0,1:T(8,128)S(1)} %copy.41, s32[128,8]{0,1:T(8,128)S(1)} %copy.42, s32[128,8]{0,1:T(8,128)} %param.8), kind=kLoop, calls=%fused_computation.18 | loop fusion | flops 9216 | bytes 16384 | tf_op jit(solution)/shard_map/jit(_where)/select_n | solution.py:38
  3.6 0.7 %convert_reduce_fusion.2 = (bf16[16,128]{1,0:T(8,128)(2,1)S(1)}, f32[16,128]{1,0:T(8,128)S(1)}) fusion(s32[128,8]{0,1:T(8,128)S(1)} %add_select_fusion, f32[128,8]{0,1:T(8,128)} %param.9), kind=kLoop, calls=%fused_computation.13 | loop fusion | flops 77824 | bytes 20480 | tf_op jit(solution)/shard_map/reduce_sum | solution.py:41
  4.3 1.5 %convolution_convert_fusion.2 = bf16[16,4096]{1,0:T(8,128)(2,1)S(1)} fusion(bf16[128,4096]{1,0:T(8,128)(2,1)} %param.7, bf16[16,128]{1,0:T(8,128)(2,1)S(1)} %get-tuple-element.2), kind=kOutput, calls=%fused_computation.2 | convolution fusion | flops 16842752 | bytes 1183744 | tf_op jit(solution)/shard_map/dot_general | solution.py:43
  5.8 13.5 %all_to_all.10 = bf16[4,16,4096]{2,1,0:T(8,128)(2,1)S(1)} all-to-all(bf16[4,16,4096]{2,1,0:T(8,128)(2,1)S(1)} %reshape.121), channel_id=1, replica_groups=mesh['ep'=4,'grp'=8] {'ep'}, dimensions={0} | all-to-all | bytes 1048576 | tf_op jit(solution)/shard_map/all_to_all | solution.py:47
  19.3 0.9 %fusion.10 = f32[64,320]{1,0:T(8,128)S(1)} fusion(bf16[64,4096]{1,0:T(8,128)(2,1)S(1)} %bitcast.17, bf16[4096,320]{0,1:T(8,128)(2,1)S(1)} %copy-done.1), kind=kOutput, calls=%fused_computation.25 | convolution fusion | flops 167772160 | bytes 3227648 | tf_op jit(solution)/shard_map/dot_general | solution.py:49
  20.3 4.7 %convolution_convert_fusion.1 = bf16[64,4096]{1,0:T(8,128)(2,1)} fusion(bf16[320,4096]{1,0:T(8,128)(2,1)S(1)} %copy-done, bf16[64,4096]{1,0:T(8,128)(2,1)S(1)} %bitcast.18, bf16[4096,320]{0,1:T(8,128)(2,1)} %param.11, f32[64,320]{1,0:T(8,128)S(1)} %fusion.10), kind=kOutput, calls=%fused_computation.1 | convolution fusion | flops 335929344 | bytes 6373376 | tf_op jit(solution)/shard_map/dot_general | solution.py:52
  25.0 3.5 %all-to-all-start.1 = ((bf16[4,16,4096]{2,1,0:T(8,128)(2,1)}), bf16[4,16,4096]{2,1,0:T(8,128)(2,1)S(1)}, u32[]{:S(2)}, u32[]{:S(2)}) async-start(bf16[4,16,4096]{2,1,0:T(8,128)(2,1)} %bitcast.19), calls=%async_computation.1 | async-start | bytes 1048576 | tf_op jit(solution)/shard_map/all_to_all | solution.py:53
  28.5 0.1 copy.43
  28.6 0.1 eq.58
  28.7 0.2 convert_reduce_fusion.1
  28.9 8.5 %all-gather.1 = f32[4,1,128]{2,1,0:T(1,128)S(1)} all-gather(f32[1,1,128]{2,1,0:T(1,128)S(1)} %bitcast.20), channel_id=2, replica_groups=mesh['ep'=4,'grp'=8] {'ep'}, dimensions={0}, use_global_device_ids=true | all-gather | bytes 2560 | tf_op jit(solution)/shard_map/all_gather | solution.py:13
  37.4 13.8 %psum.7 = f32[128]{0:T(128)S(1)} all-reduce(f32[128]{0:T(128)S(1)} %reduce_sum.57), channel_id=1, replica_groups=mesh['ep'=4,'grp'=8] {'grp'}, use_global_device_ids=true, to_apply=%region_7.8 | all-reduce | flops 128 | bytes 1024 | tf_op jit(solution)/shard_map/psum | solution.py:22
  51.2 0.5 multiply_subtract_fusion
  51.7 0.1 convert_reduce_fusion
  51.8 2.8 %convolution_convert_fusion = bf16[128,4096]{1,0:T(8,128)(2,1)} fusion(f32[16,128]{1,0:T(8,128)S(1)} %get-tuple-element.3, f32[16,4096]{1,0:T(8,128)S(1)} %convert_reduce_fusion), kind=kOutput, calls=%fused_computation | convolution fusion | flops 101187584 | bytes 1318912 | tf_op jit(solution)/shard_map/dot_general | solution.py:60
  (14 shorter events, 0.2 us)
Async XLA Ops:
  0.6 19.6 %copy-start = (bf16[320,4096]{1,0:T(8,128)(2,1)S(1)}, bf16[320,4096]{1,0:T(8,128)(2,1)}, u32[]{:S(2)}) copy-start(bf16[320,4096]{1,0:T(8,128)(2,1)} %param.12) | copy-start | bytes 7864324
  2.7 16.6 %copy-start.1 = (bf16[4096,320]{0,1:T(8,128)(2,1)S(1)}, bf16[4096,320]{0,1:T(8,128)(2,1)}, u32[]{:S(2)}) copy-start(bf16[4096,320]{0,1:T(8,128)(2,1)} %param.10) | copy-start | bytes 7864324
  20.2 8.2 %copy-start.2 = (s32[128,8]{0,1:T(8,128)S(1)}, s32[128,8]{0,1:T(8,128)}, u32[]{:S(2)}) copy-start(s32[128,8]{0,1:T(8,128)} %param.8) | copy-start | bytes 12292
  20.3 30.9 %copy-start.3 = (f32[128]{0:T(128)S(1)}, f32[128]{0:T(128)}, u32[]{:S(2)}) copy-start(f32[128]{0:T(128)} %param.13) | copy-start | bytes 1540
  25.0 26.7 %all-to-all-start.1 = ((bf16[4,16,4096]{2,1,0:T(8,128)(2,1)}), bf16[4,16,4096]{2,1,0:T(8,128)(2,1)S(1)}, u32[]{:S(2)}, u32[]{:S(2)}) async-start(bf16[4,16,4096]{2,1,0:T(8,128)(2,1)} %bitcast.19), calls=%async_computation.1 | async-start | bytes 1048576 | tf_op jit(solution)/shard_map/all_to_all | solution.py:53
